TPU v7x, 32 devices: a whole 2x2x4 slice. The times are simulated.
32 devices in a mesh: ka: 8 (over z, x), row: 4 (over y, core).
Axes of the slice: x: 2, y: 2, z: 4, core: 2. Of those that a mesh axis runs over, the one named last changes fastest.
Arguments:
- gauge: bfloat16 [32, 2, 384, 384], P(('ka', 'row')), may hold values from -3 to 3
- energies: float32 [32, 384], P(('ka', 'row')), may hold values from -5 to 5
- kmesh: int32 [3, 32], replicated, may hold values from 0 to 11
- lattice: int32 [3, 256], P(None, 'row'), may hold values from -8 to 8
- degeneracy: int32 [256], P('row'), may hold values from 1 to 8
- path: int32 [3, 8], replicated, may hold values from 0 to 63
Outputs:
- lattice_h: bfloat16 [256, 384, 768], P('row', 'ka')
- path_h: float32 [8, 384, 768], P('row', 'ka')
All inputs are finite; a program needn't handle non-finite values.
Results may differ from a plain program's by a relative error of at most 0.006.
Values may be sent and summed in bfloat16 or wider, within the bound.
No kernel may reach another device: no remote copies, remote signals or barrier semaphores. Data moves between devices by JAX's collectives and lax.ppermute only.
A program may use at most 64 MiB of HBM per device.

v0:
```python
import math

import jax
import jax.numpy as jnp
from jax import lax
from jax.sharding import PartitionSpec as P

MESH = 12
PATH_DEN = 64


def phases(vectors, coords):
    windings = jnp.mod(jnp.sum(vectors[:, :, None] * coords[:, None, :], 0), MESH)
    angles = windings.astype(jnp.float32) * (2.0 * math.pi / MESH)
    return jnp.concatenate([jnp.cos(angles), jnp.sin(angles)], 0).astype(jnp.bfloat16)


def path_factors(path_coords, vectors, counts):
    windings = jnp.mod(jnp.sum(path_coords[:, :, None] * vectors[:, None, :], 0), PATH_DEN)
    angles = windings.astype(jnp.float32) * (2.0 * math.pi / PATH_DEN)
    weights = 1.0 / counts.astype(jnp.float32)
    return jnp.concatenate(
        [jnp.cos(angles) * weights[None, :], jnp.sin(angles) * weights[None, :]], 0
    ).astype(jnp.bfloat16)


def combine_fourier(products, scale_by):
    real_part = products[0, :, :, 0] + products[1, :, :, 1]
    imag_part = products[0, :, :, 1] - products[1, :, :, 0]
    return jnp.concatenate([real_part, imag_part], -1) / scale_by


def combine_path(products):
    real_part = products[0, :, :, 0] - products[1, :, :, 1]
    imag_part = products[0, :, :, 1] + products[1, :, :, 0]
    return jnp.concatenate([real_part, imag_part], -1)


def local(gauge, energies, kmesh, lattice, degeneracy, path):
    per_device = gauge.shape[0]
    orbitals = gauge.shape[2]
    ka_count = lax.axis_size("ka")
    row_count = lax.axis_size("row")
    k_total = kmesh.shape[1]
    path_dev = path.shape[1] // row_count
    scaled = (energies[:, None, :, None] * gauge.astype(jnp.float32)).astype(jnp.bfloat16)
    stacked = jnp.concatenate([gauge[:, 0], gauge[:, 1]], 1)
    partner = jnp.concatenate(
        [
            jnp.concatenate([scaled[:, 0], scaled[:, 1]], 2),
            jnp.concatenate([scaled[:, 1], -scaled[:, 0]], 2),
        ],
        1,
    )
    rotated = jnp.einsum(
        "kna,knb->kab", stacked, partner, preferred_element_type=jnp.float32
    ).astype(jnp.bfloat16)
    arrived = lax.all_to_all(rotated, "ka", split_axis=1, concat_axis=0, tiled=True)
    local_rows = arrived.shape[1]
    lattice_rows = lattice.shape[1]
    k_order = (
        kmesh.reshape(3, ka_count, row_count, per_device).transpose(0, 2, 1, 3).reshape(3, k_total)
    )
    vectors_all, counts_all = (
        lax.all_gather(lattice, "row", axis=1, tiled=True),
        lax.all_gather(degeneracy, "row", axis=0, tiled=True),
    )
    total_vectors = vectors_all.shape[1]
    own_path = lax.dynamic_slice_in_dim(path, lax.axis_index("row") * path_dev, path_dev, 1)
    factors_path = path_factors(own_path, vectors_all, counts_all).astype(jnp.float32)
    factors_mesh = phases(vectors_all, k_order).astype(jnp.float32)
    with_cos = jnp.dot(
        factors_path,
        factors_mesh[:total_vectors],
        preferred_element_type=jnp.float32,
        precision=lax.Precision.HIGHEST,
    )
    with_sin = jnp.dot(
        factors_path,
        factors_mesh[total_vectors:],
        preferred_element_type=jnp.float32,
        precision=lax.Precision.HIGHEST,
    )
    mixing_real = (with_cos[:path_dev] + with_sin[path_dev:]) / k_total
    mixing_imag = (with_cos[path_dev:] - with_sin[:path_dev]) / k_total
    mixing = jnp.concatenate([mixing_real, mixing_imag], 0)
    k_piece = lax.all_gather(arrived, "row", axis=0, tiled=True)
    amount = k_piece.shape[0]
    fourier_amount = k_piece.shape[0]
    factors = phases(lattice, k_order)
    fourier_sum = jnp.dot(
        factors, k_piece.reshape(fourier_amount, -1), preferred_element_type=jnp.float32
    )
    path_sum = jnp.dot(
        mixing,
        k_piece.reshape(amount, -1).astype(jnp.float32),
        preferred_element_type=jnp.float32,
        precision=lax.Precision.HIGHEST,
    )
    summed, path_sum = (fourier_sum, path_sum)
    products = summed.reshape(2, lattice_rows, local_rows, 2, orbitals)
    lattice_f = combine_fourier(products, k_total)
    path_h = combine_path(path_sum.reshape(2, path_dev, local_rows, 2, orbitals))
    lattice_h = lattice_f.astype(jnp.bfloat16)
    return (lattice_h, path_h)


def solution(mesh):
    return jax.shard_map(
        local,
        mesh=mesh,
        in_specs=(
            P(("ka", "row"), None, None, None),
            P(("ka", "row"), None),
            P(),
            P(None, "row"),
            P("row"),
            P(),
        ),
        out_specs=(P("row", "ka", None), P("row", "ka", None)),
        check_vma=False,
    )
```

profile of v0, /device:TPU:0, one launch (start us, length us, event | category | flops | bytes accessed | tf_op | source)
XLA Modules:
  0.0 96.4 jit_solution(5764981165644782622)
XLA Ops:
  7.2 0.0 copy-start
  7.2 0.0 all-gather.3.cloned.1.call-start
  7.2 0.7 reduce
  7.9 1.2 %multiply_convert_fusion = bf16[1,2,384,384]{3,2,1,0:T(8,128)(2,1)S(1)} fusion(bf16[1,2,384,384]{3,2,1,0:T(8,128)(2,1)} %param.6, f32[384]{0:T(512)S(1)} %reduce), kind=kLoop, calls=%fused_computation.23 | loop fusion | flops 884736 | bytes 1181184 | tf_op jit(solution)/shard_map/convert_element_type | solution.py:46
  9.2 1.3 %slice_bitcast_fusion.3 = (bf16[1,384,384]{2,1,0:T(8,128)(2,1)S(1)}, bf16[1,384,384]{2,1,0:T(8,128)(2,1)S(1)}, bf16[1,384,384]{2,1,0:T(8,128)(2,1)S(1)}, bf16[1,384,384]{2,1,0:T(8,128)(2,1)S(1)}) fusion(bf16[1,2,384,384]{3,2,1,0:T(8,128)(2,1)S(1)} %multiply_convert_fusion, bf16[1,2,384,384]{3,2,1,0:T(8,128)(2,1)} %param.6), kind=kLoop, calls=%fused_computation.28 | loop fusion | bytes 2359296 | tf_op jit(solution)/shard_map/squeeze | solution.py:50
  10.5 0.7 fusion.10
  11.1 0.9 copy.83
  12.0 0.5 broadcast.30
  12.6 4.4 %reduce.1 = bf16[384,768]{1,0:T(8,128)(2,1)S(1)} reduce(bf16[384,1,768]{2,1,0:T(2,128)(2,1)S(1)} %bitcast.83, bf16[]{:T(256)} %broadcast.30), dimensions={1}, to_apply=%bitcast.81.reduce_sub_computation | reduce | bytes 1179650
  16.9 0.1 reshape.77
  17.1 23.6 %all_to_all.12 = bf16[8,2,18432]{2,1,0:T(2,128)(2,1)S(1)} all-to-all(bf16[8,2,18432]{2,1,0:T(2,128)(2,1)S(1)} %reshape.77), channel_id=1, replica_groups=mesh['ka'=8,'row'=4] {'ka'}, dimensions={0} | all-to-all | bytes 1179648 | tf_op jit(solution)/shard_map/all_to_all | solution.py:58
  40.7 0.0 copy-start.1
  40.7 0.0 copy-start.2
  40.7 0.0 copy-start.4
  40.7 0.0 copy-start.3
  40.7 0.6 reshape.78
  41.3 0.9 copy.66
  42.2 0.0 all-gather.3.cloned.1.call-update
  42.2 0.0 copy-done.1
  42.2 5.2 %all-gather = s32[4,64,3]{1,2,0:T(4,128)S(1)} all-gather(s32[1,64,3]{1,2,0:T(4,128)S(1)} %bitcast.92), channel_id=1, replica_groups=mesh['ka'=8,'row'=4] {'row'}, dimensions={0}, use_global_device_ids=true | all-gather | bytes 3840 | tf_op jit(solution)/shard_map/all_gather | solution.py:65
  47.4 0.1 reshape.69
  47.5 0.0 copy-done.2
  47.5 0.1 reshape.61
  47.6 0.1 copy.50
  47.7 0.1 mul.87
  47.8 0.1 multiply_reduce_fusion.1
  47.9 0.1 cosine_convert_fusion.1
  47.9 0.1 pad_maximum_fusion.1
  48.0 0.1 convert_element_type.44
  48.1 0.0 copy-done.4
  48.1 0.6 dynamic-slice
  49.4 0.0 copy-done.3
  49.4 0.2 dynamic-update-slice
  49.6 5.2 %all-reduce = s32[256]{0:T(256)S(1)} all-reduce(s32[256]{0:T(256)S(1)} %dynamic-update-slice), channel_id=1, replica_groups=mesh['ka'=8,'row'=4] {'row'}, use_global_device_ids=true, to_apply=%add | all-reduce | flops 256 | bytes 2048
  54.8 0.0 copy-done
  54.8 0.1 constant_dynamic-slice_fusion
  54.9 0.1 multiply_reduce_fusion
  54.9 0.1 multiply_reduce_fusion.2
  55.0 0.1 multiply_convert_fusion.2
  55.1 0.1 multiply_convert_fusion.1
  55.2 0.3 fusion.28
  55.4 0.3 fusion.27
  55.7 9.2 %all-gather.3.cloned.1.call-done = bf16[32,48,768]{2,1,0:T(8,128)(2,1)} async-done(((bf16[8,48,768]{2,1,0:T(8,128)(2,1)}), bf16[32,48,768]{2,1,0:T(8,128)(2,1)}) %all-gather.3.cloned.1.call-update) | async-done | bytes 2359312 | tf_op jit(solution)/shard_map/all_gather | solution.py:87
  64.9 3.8 %copy.71 = bf16[4,8,48,768]{3,1,2,0:T(8,128)(2,1)} copy(bf16[4,8,48,768]{3,2,1,0:T(8,128)(2,1)} %bitcast.86) | data formatting | bytes 4718592
  68.8 3.5 %dot_general.23 = bf16[48,2,384,32]{2,1,0,3:T(2,128)(2,1)S(1)} reshape(bf16[36864,32]{0,1:T(8,128)(2,1)} %bitcast.82) | data formatting | bytes 4718592 | tf_op jit(solution)/shard_map/dot_general | solution.py:91
  72.3 1.5 %fusion.4 = f32[2,2,48,2,384]{4,1,3,2,0:T(2,128)S(1)} fusion(f32[2,2,32,1,1]{2,1,4,3,0:T(2,128)S(1)} %bitcast.91, bf16[48,2,384,32]{2,1,0,3:T(2,128)(2,1)S(1)} %dot_general.23), kind=kOutput, calls=%fused_computation.8 | convolution fusion | flops 56623104 | bytes 2949632 | tf_op jit(solution)/shard_map/dot_general | solution.py:94
  73.8 0.1 fusion.19
  73.9 0.1 fusion.21
  74.0 2.6 %fusion.6 = f32[2,64,48,2,384]{4,1,3,2,0:T(8,128)S(1)} fusion(bf16[48,2,384,32]{2,1,0,3:T(2,128)(2,1)S(1)} %dot_general.23, bf16[2,64,32,1,1]{1,0,2,4,3:T(2,128)(2,1)S(1)} %bitcast.87), kind=kOutput, calls=%fused_computation.10 | convolution fusion | flops 301989888 | bytes 21241856 | tf_op jit(solution)/shard_map/dot_general | solution.py:91
  76.6 0.8 fusion.1
  77.4 0.8 fusion.3
  78.2 0.1 pad_maximum_fusion
  78.3 0.7 copy.61
  79.1 3.3 %fusion = bf16[64,48,768]{2,0,1:T(8,128)(2,1)} fusion(f32[64,48,384]{2,0,1:T(8,128)S(1)} %fusion.1, f32[64,48,384]{2,0,1:T(8,128)S(1)} %fusion.3), kind=kLoop, calls=%fused_computation.1 | loop fusion | flops 7077888 | bytes 14155776 | tf_op jit(solution)/shard_map/convert_element_type | solution.py:104
  82.4 7.1 %copy.60 = bf16[64,48,768]{2,1,0:T(8,128)(2,1)} copy(bf16[64,48,768]{2,0,1:T(8,128)(2,1)} %fusion) | data formatting | bytes 9437184
  (6 shorter events, 0.1 us)
Async XLA Ops:
  7.2 47.6 %copy-start = (s32[3,8]{1,0:T(4,128)S(1)}, s32[3,8]{1,0:T(4,128)}, u32[]{:S(2)}) copy-start(s32[3,8]{1,0:T(4,128)} %param.11) | copy-start | bytes 292
  7.2 57.8 %all-gather.3.cloned.1.call-start = ((), (), s32[]{:S(2)}) async-start(), calls=%async_computation.1 | async-start | bytes 2949120 | tf_op jit(solution)/shard_map/all_gather | solution.py:87
  40.7 1.5 %copy-start.1 = (s32[3,64]{1,0:T(4,128)S(1)}, s32[3,64]{1,0:T(4,128)}, u32[]{:S(2)}) copy-start(s32[3,64]{1,0:T(4,128)} %param.9) | copy-start | bytes 2308
  40.7 6.8 %copy-start.2 = (s32[3,32]{1,0:T(4,128)S(1)}, s32[3,32]{1,0:T(4,128)}, u32[]{:S(2)}) copy-start(s32[3,32]{1,0:T(4,128)} %param.8) | copy-start | bytes 1156
  40.7 7.4 %copy-start.4 = (u32[32]{0:T(128)S(1)}, u32[32]{0:T(128)}, u32[]{:S(2)}) copy-start(u32[32]{0:T(128)} %constant.58) | copy-start | bytes 388
  40.7 8.7 %copy-start.3 = (s32[64]{0:T(128)S(1)}, s32[64]{0:T(128)}, u32[]{:S(2)}) copy-start(s32[64]{0:T(128)} %param.10) | copy-start | bytes 772
Sparse Core Ops, SparseCore 0:
  42.3 22.5 all-gather.2
where the time goes:
time: 96.8 us; the launch traced here: 96.4 us
  blocking collectives  34 us (35%)
  local copies, waits for them, and re-layouts  20.9 us (22%)
  between operations  14.9 us (15%)
  other arithmetic  12 us (12%)
  waiting for transfers between devices  9.25 us (10%)
  matrix products  5.35 us (6%)
    all_to_all x1, blocking collectives, local(): lax.all_to_all(rotated, 'ka', split_axis=1, concat_axis=0, tiled=True)  23.6 us
    unnamed x21, local copies, waits for them, and re-layouts  14.8 us
    all_gather x1, waiting for transfers between devices, local(): k_piece = lax.all_gather(arrived, 'row', axis=0, tiled=True)  9.23 us
    all_gather x1, blocking collectives, local(): lax.all_gather(lattice, 'row', axis=1, tiled=True)  5.19 us
    unnamed x1, blocking collectives  5.15 us
    unnamed x2, other arithmetic  5.07 us
    dot_general x1, local copies, waits for them, and re-layouts, local(): jnp.dot(factors, k_piece.reshape(fourier_amount, -1), preferred_element_t...  3.51 us
    convert_element_type x1, other arithmetic, local(): lattice_h = lattice_f.astype(jnp.bfloat16)  3.29 us
  transfers between devices with their start and end apart: 1, of which 1 were waited for; matrix products, arithmetic and copies ran while one was open for 2% of the time, Pallas kernels for 0%

commit v1 on v0

v1 whole, which is shorter than its diff:
```python
import functools
import math

import jax
import jax.numpy as jnp
from jax import lax
from jax.experimental import pallas as pl
from jax.experimental.pallas import tpu as pltpu
from jax.sharding import PartitionSpec as P

MESH = 12
PATH_DEN = 64
SUB = 8


def rotate_kernel(gauge_ref, energy_ref, out_ref):
    orbitals = gauge_ref.shape[-1]
    bands = gauge_ref.shape[-2]
    for k in range(gauge_ref.shape[0]):
        energy = jnp.broadcast_to(energy_ref[k : k + 1, :], (SUB, bands)).T[:, :1]
        ur, ui = gauge_ref[k, 0], gauge_ref[k, 1]
        sr = (energy * ur.astype(jnp.float32)).astype(jnp.bfloat16)
        si = (energy * ui.astype(jnp.float32)).astype(jnp.bfloat16)
        contract = lambda a, b: lax.dot_general(
            a, b, (((0,), (0,)), ((), ())), preferred_element_type=jnp.float32
        )
        out_ref[k, :, :orbitals] = (contract(ur, sr) + contract(ui, si)).astype(jnp.bfloat16)
        out_ref[k, :, orbitals:] = (contract(ur, si) - contract(ui, sr)).astype(jnp.bfloat16)


def transform_kernel(scale_by, lattice_count, path_count, pieces, *refs):
    piece_refs = refs[:pieces]
    with_real_ref, with_imag_ref, lattice_ref, path_ref = refs[pieces:]
    orbitals = lattice_ref.shape[-1] // 2
    first = pl.multiple_of(pl.program_id(0) * SUB, SUB)
    blocks = [
        ref[:, pl.ds(first, SUB), :].astype(jnp.float32).reshape(-1, 2 * orbitals) for ref in piece_refs
    ]
    block = jnp.concatenate(blocks, 0).astype(jnp.bfloat16)
    real, imag = block[:, :orbitals], block[:, orbitals:]

    def rows(start, count):
        lo, hi = start * SUB, (start + count) * SUB
        total = jnp.dot(with_real_ref[lo:hi, :], real, preferred_element_type=jnp.float32)
        total += jnp.dot(with_imag_ref[lo:hi, :], imag, preferred_element_type=jnp.float32)
        return total.reshape(count, SUB, orbitals)

    step = math.gcd(lattice_count, 16)
    for start in range(0, lattice_count, step):
        lattice_ref[start : start + step, :, :orbitals] = (rows(start, step) / scale_by).astype(jnp.bfloat16)
        lattice_ref[start : start + step, :, orbitals:] = (
            rows(lattice_count + start, step) / scale_by
        ).astype(jnp.bfloat16)
    values = rows(2 * lattice_count, 4 * path_count)
    path_ref[:, :, :orbitals] = values[:path_count] + values[2 * path_count : 3 * path_count]
    path_ref[:, :, orbitals:] = values[path_count : 2 * path_count] + values[3 * path_count :]


def cos_sin(windings, period):
    angles = windings.astype(jnp.float32) * (2.0 * math.pi / period)
    return jnp.cos(angles), jnp.sin(angles)


def mesh_phases(vectors, coords):
    windings = jnp.mod(jnp.sum(vectors[:, :, None] * coords[:, None, :], 0), MESH)
    cos, sin = cos_sin(windings, MESH)
    return cos.astype(jnp.bfloat16), sin.astype(jnp.bfloat16)


def spread(table):
    count, width = table.shape
    down = lax.broadcasted_iota(jnp.int32, (count * SUB, count), 0) // SUB
    pick = (down == lax.broadcasted_iota(jnp.int32, (count * SUB, count), 1)).astype(jnp.bfloat16)
    along = lax.broadcasted_iota(jnp.int32, (width, width * SUB), 1) // SUB
    place = (along == lax.broadcasted_iota(jnp.int32, (width, width * SUB), 0)).astype(jnp.bfloat16)
    tall = jnp.dot(pick, table, preferred_element_type=jnp.float32).astype(jnp.bfloat16)
    wide = jnp.dot(tall, place, preferred_element_type=jnp.float32)
    lane = lax.broadcasted_iota(jnp.int32, wide.shape, 1) % SUB
    sublane = lax.broadcasted_iota(jnp.int32, wide.shape, 0) % SUB
    return jnp.where(lane == sublane, wide, 0.0).astype(jnp.bfloat16)


def flip(array, axis, mask, size):
    return lax.ppermute(array, axis, [(i, i ^ mask) for i in range(size)])


def local(gauge, energies, kmesh, lattice, degeneracy, path):
    per_device, _, _, orbitals = gauge.shape
    ka_count = lax.axis_size("ka")
    row_count = lax.axis_size("row")
    row = lax.axis_index("row")
    k_total = kmesh.shape[1]
    lattice_count = lattice.shape[1]
    path_count = path.shape[1] // row_count
    local_rows = orbitals // ka_count
    vmem = pl.BlockSpec(memory_space=pltpu.VMEM)

    rotated = pl.pallas_call(
        rotate_kernel,
        out_shape=jax.ShapeDtypeStruct((per_device, orbitals, 2 * orbitals), jnp.bfloat16),
        in_specs=[vmem, vmem],
        out_specs=vmem,
        name="rotate",
    )(gauge, energies)
    arrived = lax.all_to_all(rotated, "ka", split_axis=1, concat_axis=0, tiled=True)

    pieces, offsets = [arrived], [0]
    table = jnp.concatenate([lattice, degeneracy[None, :]], 0)
    mask = row_count // 2
    while mask:
        pieces = pieces + [flip(piece, "row", mask, row_count) for piece in pieces]
        offsets = offsets + [offset ^ mask for offset in offsets]
        table = jnp.concatenate([table, flip(table, "row", mask, row_count)], 1)
        mask //= 2

    by_device = kmesh.reshape(3, ka_count, row_count, per_device)
    coords = jnp.concatenate(
        [
            lax.dynamic_index_in_dim(by_device, row ^ offset, 2, keepdims=False).reshape(3, -1)
            for offset in offsets
        ],
        1,
    )
    cosf, sinf = mesh_phases(lattice, coords)
    vectors_all, counts_all = table[:3], table[3]
    cosf_all, sinf_all = mesh_phases(vectors_all, coords)
    own_path = lax.dynamic_slice_in_dim(path, row * path_count, path_count, 1)
    windings = jnp.mod(jnp.sum(own_path[:, :, None] * vectors_all[:, None, :], 0), PATH_DEN)
    cosp, sinp = cos_sin(windings, PATH_DEN)
    weights = 1.0 / counts_all.astype(jnp.float32)
    factors = jnp.concatenate([cosp * weights, sinp * weights], 0).astype(jnp.bfloat16)
    with_cos = jnp.dot(factors, cosf_all, preferred_element_type=jnp.float32)
    with_sin = jnp.dot(factors, sinf_all, preferred_element_type=jnp.float32)
    mixing_real = (with_cos[:path_count] + with_sin[path_count:]) / k_total
    mixing_imag = (with_cos[path_count:] - with_sin[:path_count]) / k_total
    times_real = jnp.concatenate([mixing_real, mixing_imag], 0)
    times_imag = jnp.concatenate([-mixing_imag, mixing_real], 0)

    def halves(values):
        high = lax.reduce_precision(values, 8, 7)
        return [high.astype(jnp.bfloat16), (values - high).astype(jnp.bfloat16)]

    with_real = spread(jnp.concatenate([cosf, -sinf] + halves(times_real), 0))
    with_imag = spread(jnp.concatenate([sinf, cosf] + halves(times_imag), 0))

    return pl.pallas_call(
        functools.partial(transform_kernel, k_total, lattice_count, path_count, len(pieces)),
        grid=(local_rows // SUB,),
        out_shape=(
            jax.ShapeDtypeStruct((lattice_count, local_rows, 2 * orbitals), jnp.bfloat16),
            jax.ShapeDtypeStruct((path_count, local_rows, 2 * orbitals), jnp.float32),
        ),
        in_specs=[vmem] * (len(pieces) + 2),
        out_specs=(
            pl.BlockSpec((lattice_count, SUB, 2 * orbitals), lambda i: (0, i, 0)),
            pl.BlockSpec((path_count, SUB, 2 * orbitals), lambda i: (0, i, 0)),
        ),
        name="transform",
    )(*pieces, with_real, with_imag)


def solution(mesh):
    return jax.shard_map(
        local,
        mesh=mesh,
        in_specs=(
            P(("ka", "row"), None, None, None),
            P(("ka", "row"), None),
            P(),
            P(None, "row"),
            P("row"),
            P(),
        ),
        out_specs=(P("row", "ka", None), P("row", "ka", None)),
        check_vma=False,
    )
```

time: 96.8 us -> 65.2 us (0.67)
  blocking collectives: 34 us -> 0 us
  waiting for transfers between devices: 9.25 us -> 26.4 us
  local copies, waits for them, and re-layouts: 20.9 us -> 6.75 us
  between operations: 14.9 us -> 0.81 us
  Pallas kernels: 0 us -> 10.5 us
  starting transfers between devices: 0.04 us -> 9.4 us
  other arithmetic: 12 us -> 5.99 us
    all_to_all x1 -> x0, blocking collectives: 23.6 us -> none  [local(): lax.all_to_all(rotated, 'ka', split_axis=1, concat_axis=0, tiled=True)]
    ppermute x0 -> x5, waiting for transfers between devices: none -> 13.4 us  [flip(): return lax.ppermute(array, axis, [(i, i ^ mask) for i in range(size)])]
    all_to_all x0 -> x1, waiting for transfers between devices: none -> 13 us  [local(): lax.all_to_all(rotated, 'ka', split_axis=1, concat_axis=0, tiled=True)]
    unnamed x21 -> x20, local copies, waits for them, and re-layouts: 14.8 us -> 3.85 us
    pallas_call x0 -> x2, Pallas kernels: none -> 10.5 us  [the longest x1 7.5 us: local(): pl.pallas_call(functools.partial(transform_kernel, k_total, lattice_count...]
    all_gather x1 -> x0, waiting for transfers between devices: 9.23 us -> none  [local(): k_piece = lax.all_gather(arrived, 'row', axis=0, tiled=True)]
    all_to_all x0 -> x1, starting transfers between devices: none -> 5.81 us  [local(): lax.all_to_all(rotated, 'ka', split_axis=1, concat_axis=0, tiled=True)]
    all_gather x1 -> x0, blocking collectives: 5.19 us -> none  [local(): lax.all_gather(lattice, 'row', axis=1, tiled=True)]
  transfers between devices with their start and end apart: 1 -> 6, of which waited for: 1 -> 3; matrix products, arithmetic and copies ran while one was open for 2% -> 22% of each run, Pallas kernels for 0% -> 5%
where the time goes in v1:
time: 65.2 us; the launch traced here: 64.7 us
  waiting for transfers between devices  26.4 us (40%)
  Pallas kernels  10.5 us (16%)
  starting transfers between devices  9.4 us (14%)
  local copies, waits for them, and re-layouts  6.75 us (10%)
  other arithmetic  5.99 us (9%)
  matrix products  4.86 us (7%)
  between operations  0.81 us (1%)
    ppermute x5, waiting for transfers between devices, flip(): return lax.ppermute(array, axis, [(i, i ^ mask) for i in range(size)])  13.4 us
    all_to_all x1, waiting for transfers between devices, local(): lax.all_to_all(rotated, 'ka', split_axis=1, concat_axis=0, tiled=True)  13 us
    pallas_call x1, Pallas kernels, local(): pl.pallas_call(functools.partial(transform_kernel, k_total, lattice_count...  7.5 us
    all_to_all x1, starting transfers between devices, local(): lax.all_to_all(rotated, 'ka', split_axis=1, concat_axis=0, tiled=True)  5.81 us
    unnamed x1, other arithmetic  4.37 us
    dot_general x2, matrix products, spread(): wide = jnp.dot(tall, place, preferred_element_type=jnp.float32)  4.34 us
    unnamed x20, local copies, waits for them, and re-layouts  3.85 us
    ppermute x5, starting transfers between devices, flip(): return lax.ppermute(array, axis, [(i, i ^ mask) for i in range(size)])  3.59 us
  transfers between devices with their start and end apart: 6, of which 3 were waited for; matrix products, arithmetic and copies ran while one was open for 22% of the time, Pallas kernels for 5%

profile of v1, /device:TPU:0, one launch (start us, length us, event | category | flops | bytes accessed | tf_op | source)
XLA Modules:
  0.0 64.7 jit_solution(5419120922653542861)
XLA Ops:
  0.6 0.0 copy-start
  0.6 0.7 %pad_add_fusion.2 = s32[4,64]{1,0:T(4,128)S(1)} fusion(s32[1,64]{1,0:T(1,128)} %bitcast.17, s32[3,64]{1,0:T(4,128)} %param.9), kind=kLoop, calls=%fused_computation.78 | loop fusion | flops 256 | bytes 2048 | tf_op jit(solution)/shard_map/concatenate | solution.py:108
  1.4 3.0 %collective-permute-start.3 = (s32[4,64]{1,0:T(4,128)S(1)}, s32[4,64]{1,0:T(4,128)S(1)}, u32[]{:S(2)}, u32[]{:S(2)}) collective-permute-start(s32[4,64]{1,0:T(4,128)S(1)} %pad_add_fusion.2), channel_id=1, source_target_pairs={{0,2},{1,3},{2,0},{3,1},{4,6},{5,7},{6,4},{7,5},{8,10},{9,11},{10,... | collective-permute-start | bytes 3080 | tf_op jit(solution)/shard_map/ppermute | solution.py:84
  4.4 3.0 %rotate.1 = bf16[1,384,768]{2,1,0:T(8,128)(2,1)} custom-call(bf16[1,2,384,384]{3,2,1,0:T(8,128)(2,1)} %gauge_ref.1, f32[1,384]{1,0:T(1,128)} %energy_ref.1), custom_call_target="tpu_custom_call" | custom-call | tf_op jit(solution)/shard_map/rotate/pallas_call | solution.py:98
  7.4 2.0 %copy.25 = bf16[1,384,768]{2,0,1:T(2,128)(2,1)S(1)} copy(bf16[1,384,768]{2,1,0:T(8,128)(2,1)} %rotate.1) | data formatting | bytes 1179648 | tf_op jit(solution)/shard_map/rotate/pallas_call | solution.py:98
  9.3 0.5 broadcast.113
  9.9 4.4 %reduce.8 = bf16[384,768]{1,0:T(8,128)(2,1)S(1)} reduce(bf16[384,1,768]{2,1,0:T(2,128)(2,1)S(1)} %bitcast.8, bf16[]{:T(256)} %broadcast.113), dimensions={1}, to_apply=%bitcast.6.reduce_sub_computation | reduce | bytes 1179650
  14.2 0.0 copy-start.7
  14.2 0.0 copy-start.5
  14.3 0.0 copy-start.6
  14.3 1.0 %reshape.40 = bf16[8,2,18432]{2,1,0:T(2,128)(2,1)} reshape(bf16[384,768]{1,0:T(8,128)(2,1)S(1)} %reduce.8) | data formatting | bytes 1179648
  15.2 5.8 %all-to-all-start = ((bf16[8,2,18432]{2,1,0:T(2,128)(2,1)}), bf16[8,2,18432]{2,1,0:T(2,128)(2,1)S(1)}, u32[]{:S(2)}, u32[]{:S(2)}) async-start(bf16[8,2,18432]{2,1,0:T(2,128)(2,1)} %reshape.40), calls=%async_computation | async-start | bytes 1179648 | tf_op jit(solution)/shard_map/all_to_all | solution.py:105
  21.1 0.0 copy-done.7
  21.1 0.1 reshape.31
  21.1 0.4 dynamic-slice_reduce_fusion.3
  21.5 0.1 pad_add_fusion.1
  21.6 0.0 copy-done.5
  21.6 0.1 multiply_reduce_fusion.1
  21.7 0.1 cosine_convert_fusion.1
  21.8 0.1 fusion.81
  21.9 0.0 copy-done
  21.9 0.1 constant_dynamic-slice_fusion
  22.0 0.0 collective-permute-done.3
  22.0 0.0 copy-done.6
  22.0 0.1 pad_add_fusion.3
  22.1 0.0 collective-permute-start.4
  22.1 1.1 %collective-permute-done.4 = s32[4,128]{1,0:T(4,128)S(1)} collective-permute-done((s32[4,128]{1,0:T(4,128)S(1)}, s32[4,128]{1,0:T(4,128)S(1)}, u32[]{:S(2)}, u32[]{:S(2)}) %collective-permute-start.4) | collective-permute-done | bytes 2080 | tf_op jit(solution)/shard_map/ppermute | solution.py:84
  23.2 0.1 fusion.67
  23.3 0.1 pad_add_fusion
  23.4 0.1 multiply_reduce_fusion
  23.5 0.1 multiply_reduce_fusion.2
  23.6 0.1 multiply_convert_fusion.1
  23.6 0.1 multiply_convert_fusion
  23.7 13.0 %all-to-all-done = bf16[8,2,18432]{2,1,0:T(2,128)(2,1)S(1)} async-done(((bf16[8,2,18432]{2,1,0:T(2,128)(2,1)}), bf16[8,2,18432]{2,1,0:T(2,128)(2,1)S(1)}, u32[]{:S(2)}, u32[]{:S(2)}) %all-to-all-start) | async-done | bytes 589856 | tf_op jit(solution)/shard_map/all_to_all | solution.py:105
  36.6 0.6 reshape.41
  37.2 0.1 copy.23
  37.3 0.0 copy-start.1
  37.3 0.6 collective-permute-start
  37.9 0.3 fusion.51
  38.1 0.3 fusion.50
  38.4 0.0 collective-permute-start.1
  38.4 12.3 %collective-permute-done.refs_1_ = bf16[8,48,768]{2,1,0:T(8,128)(2,1)S(1)} collective-permute-done((bf16[8,48,768]{2,1,0:T(8,128)(2,1)S(1)}, bf16[8,48,768]{2,1,0:T(8,128)(2,1)S(1)}, u32[]{:S(2)}, u32[]{:S(2)}) %collective-permute-start) | collective-permute-done | bytes 589856 | tf_op jit(solution)/shard_map/ppermute | solution.py:84
  50.7 0.0 copy-start.2
  50.7 0.0 collective-permute-start.2
  50.8 0.1 copy.21
  50.9 0.1 copy.22
  51.0 0.1 copy.20
  51.1 0.1 copy.19
  51.2 2.2 %fusion.refs_4_ = bf16[1088,256]{1,0:T(8,128)(2,1)} fusion(s32[1088]{0:T(1024)S(1)} %get-tuple-element.21, s32[1088]{0:T(1024)S(1)} %get-tuple-element.24, s32[1088]{0:T(1024)S(1)} %get-tuple-element.22, s32[1088]{0:T(1024)S(1)} %get-tuple-element.23, s32[256]{0:T(256)S(1)} %get-tuple-element.28, s32[256]{0:T(256)S(1)} %get-tuple-element.29, ...), kind=kOutput, calls=%fused_computation.2 | convolution fusion | flops 29070336 | bytes 589952 | tf_op jit(solution)/shard_map/dot_general | solution.py:77
  53.3 0.0 copy-done.1
  53.3 0.0 copy-done.2
  53.3 2.2 %fusion.1.refs_5_ = bf16[1088,256]{1,0:T(8,128)(2,1)} fusion(s32[1088]{0:T(1024)S(1)} %get-tuple-element.21, s32[1088]{0:T(1024)S(1)} %get-tuple-element.24, s32[1088]{0:T(1024)S(1)} %get-tuple-element.22, s32[1088]{0:T(1024)S(1)} %get-tuple-element.23, s32[256]{0:T(256)S(1)} %get-tuple-element.28, s32[256]{0:T(256)S(1)} %get-tuple-element.29, ...), kind=kOutput, calls=%fused_computation.3 | convolution fusion | flops 29070336 | bytes 589952 | tf_op jit(solution)/shard_map/dot_general | solution.py:77
  55.5 0.0 collective-permute-done.1.refs_2_
  55.5 0.0 copy-start.3
  55.5 0.0 collective-permute-done.2.refs_3_
  55.5 0.9 %copy-done.3 = bf16[8,48,768]{2,1,0:T(8,128)(2,1)} copy-done((bf16[8,48,768]{2,1,0:T(8,128)(2,1)}, bf16[8,48,768]{2,1,0:T(8,128)(2,1)S(1)}, u32[]{:S(2)}) %copy-start.3) | copy-done | bytes 589848
  56.4 0.0 copy-start.4
  56.4 0.8 %copy-done.4 = bf16[8,48,768]{2,1,0:T(8,128)(2,1)} copy-done((bf16[8,48,768]{2,1,0:T(8,128)(2,1)}, bf16[8,48,768]{2,1,0:T(8,128)(2,1)S(1)}, u32[]{:S(2)}) %copy-start.4) | copy-done | bytes 589848
  57.2 7.5 %transform.1 = (bf16[64,48,768]{2,1,0:T(8,128)(2,1)}, f32[2,48,768]{2,1,0:T(8,128)}) custom-call(bf16[8,48,768]{2,1,0:T(8,128)(2,1)} %bitcast.12, bf16[8,48,768]{2,1,0:T(8,128)(2,1)} %copy-done.2, bf16[8,48,768]{2,1,0:T(8,128)(2,1)} %copy-done.3, bf16[8,48,768]{2,1,0:T(8,128)(2,1)} %copy-done.4, bf16[1088,256]{1,0:T(8,128)(2,1)} %fusion.refs_4_, ...), custom_call_target="tpu_custom_call" | custom-call | tf_op jit(solution)/shard_map/transform/pallas_call | solution.py:146
  (8 shorter events, 0.1 us)
Async XLA Ops:
  0.6 21.3 %copy-start = (s32[3,8]{1,0:T(4,128)S(1)}, s32[3,8]{1,0:T(4,128)}, u32[]{:S(2)}) copy-start(s32[3,8]{1,0:T(4,128)} %param.11) | copy-start | bytes 292
  1.4 20.6 %collective-permute-start.3 = (s32[4,64]{1,0:T(4,128)S(1)}, s32[4,64]{1,0:T(4,128)S(1)}, u32[]{:S(2)}, u32[]{:S(2)}) collective-permute-start(s32[4,64]{1,0:T(4,128)S(1)} %pad_add_fusion.2), channel_id=1, source_target_pairs={{0,2},{1,3},{2,0},{3,1},{4,6},{5,7},{6,4},{7,5},{8,10},{9,11},{10,... | collective-permute-start | bytes 3080 | tf_op jit(solution)/shard_map/ppermute | solution.py:84
  14.2 6.8 %copy-start.7 = (s32[3,32]{1,0:T(4,128)S(1)}, s32[3,32]{1,0:T(4,128)}, u32[]{:S(2)}) copy-start(s32[3,32]{1,0:T(4,128)} %param.8) | copy-start | bytes 1156
  14.2 7.4 %copy-start.5 = (s32[3,64]{1,0:T(4,128)S(1)}, s32[3,64]{1,0:T(4,128)}, u32[]{:S(2)}) copy-start(s32[3,64]{1,0:T(4,128)} %param.9) | copy-start | bytes 2308
  14.3 7.7 %copy-start.6 = (s32[64]{0:T(128)S(1)}, s32[64]{0:T(128)}, u32[]{:S(2)}) copy-start(s32[64]{0:T(128)} %param.10) | copy-start | bytes 772
  15.2 21.4 %all-to-all-start = ((bf16[8,2,18432]{2,1,0:T(2,128)(2,1)}), bf16[8,2,18432]{2,1,0:T(2,128)(2,1)S(1)}, u32[]{:S(2)}, u32[]{:S(2)}) async-start(bf16[8,2,18432]{2,1,0:T(2,128)(2,1)} %reshape.40), calls=%async_computation | async-start | bytes 1179648 | tf_op jit(solution)/shard_map/all_to_all | solution.py:105
  22.1 1.2 %collective-permute-start.4 = (s32[4,128]{1,0:T(4,128)S(1)}, s32[4,128]{1,0:T(4,128)S(1)}, u32[]{:S(2)}, u32[]{:S(2)}) collective-permute-start(s32[4,128]{1,0:T(4,128)S(1)} %pad_add_fusion.3), channel_id=1, source_target_pairs={{0,1},{1,0},{2,3},{3,2},{4,5},{5,4},{6,7},{7,6},{8,9},{9,8},{10,11... | collective-permute-start | bytes 6152 | tf_op jit(solution)/shard_map/ppermute | solution.py:84
  37.3 16.0 %copy-start.1 = (bf16[1,384,768]{2,1,0:T(8,128)(2,1)}, bf16[1,384,768]{2,1,0:T(8,128)(2,1)S(1)}, u32[]{:S(2)}) copy-start(bf16[1,384,768]{2,1,0:T(8,128)(2,1)S(1)} %copy.23) | copy-start | bytes 1769476
  37.3 13.4 %collective-permute-start = (bf16[8,48,768]{2,1,0:T(8,128)(2,1)S(1)}, bf16[8,48,768]{2,1,0:T(8,128)(2,1)S(1)}, u32[]{:S(2)}, u32[]{:S(2)}) collective-permute-start(bf16[8,48,768]{2,1,0:T(8,128)(2,1)S(1)} %bitcast.10), channel_id=1, source_target_pairs={{0,2},{1,3},{2,0},{3,1},{4,6},{5,7},{6,4},{7,5},{8,10},{9,11},{10,... | collective-permute-start | bytes 1769480 | tf_op jit(solution)/shard_map/ppermute | solution.py:84
  38.4 17.1 %collective-permute-start.1 = (bf16[8,48,768]{2,1,0:T(8,128)(2,1)S(1)}, bf16[8,48,768]{2,1,0:T(8,128)(2,1)S(1)}, u32[]{:S(2)}, u32[]{:S(2)}) collective-permute-start(bf16[8,48,768]{2,1,0:T(8,128)(2,1)S(1)} %bitcast.11), channel_id=1, source_target_pairs={{0,1},{1,0},{2,3},{3,2},{4,5},{5,4},{6,7},{7,6},{8,9},{9,8},{10,11... | collective-permute-start | bytes 1769480 | tf_op jit(solution)/shard_map/ppermute | solution.py:84
  50.7 2.6 %copy-start.2 = (bf16[8,48,768]{2,1,0:T(8,128)(2,1)}, bf16[8,48,768]{2,1,0:T(8,128)(2,1)S(1)}, u32[]{:S(2)}) copy-start(bf16[8,48,768]{2,1,0:T(8,128)(2,1)S(1)} %collective-permute-done.refs_1_) | copy-start | bytes 1769476
  50.7 4.8 %collective-permute-start.2 = (bf16[8,48,768]{2,1,0:T(8,128)(2,1)S(1)}, bf16[8,48,768]{2,1,0:T(8,128)(2,1)S(1)}, u32[]{:S(2)}, u32[]{:S(2)}) collective-permute-start(bf16[8,48,768]{2,1,0:T(8,128)(2,1)S(1)} %collective-permute-done.refs_1_), channel_id=1, source_target_pairs={{0,1},{1,0},{2,3},{3,2},{4,5},{5,4},{6,7},{7,6},{8,9},{9,8},{10,11... | collective-permute-start | bytes 1769480 | tf_op jit(solution)/shard_map/ppermute | solution.py:84
  55.5 0.9 %copy-start.3 = (bf16[8,48,768]{2,1,0:T(8,128)(2,1)}, bf16[8,48,768]{2,1,0:T(8,128)(2,1)S(1)}, u32[]{:S(2)}) copy-start(bf16[8,48,768]{2,1,0:T(8,128)(2,1)S(1)} %collective-permute-done.1.refs_2_) | copy-start | bytes 1769476
  56.4 0.8 %copy-start.4 = (bf16[8,48,768]{2,1,0:T(8,128)(2,1)}, bf16[8,48,768]{2,1,0:T(8,128)(2,1)S(1)}, u32[]{:S(2)}) copy-start(bf16[8,48,768]{2,1,0:T(8,128)(2,1)S(1)} %collective-permute-done.2.refs_3_) | copy-start | bytes 1769476
